TPU v7x, 256 devices: a 8x8x2 block of a 8x8x16 slice. The times are simulated.
256 devices in a mesh: img: 2 (over z), ga: 16 (over y, core), band: 8 (over x).
Axes of the slice: x: 8, y: 8, z: 2, core: 2. Of those that a mesh axis runs over, the one named last changes fastest.
The devices are a block of a 8x8x16 slice.
Arguments:
- orbitals: bfloat16 [1536, 49152], P(('img', 'band'), 'ga'), parts along dimension 0, as said below
- kernel: float32 [49152], P('ga'), may hold values from 0.3 to 3
- block_vectors: bfloat16 [512, 49152], P(('img', 'band'), 'ga'), parts along dimension 0
Outputs:
- ace_vectors: bfloat16 [1536, 49152], P(('img', 'band'), 'ga'), parts along dimension 0
- exchange_block: bfloat16 [512, 49152], P(('img', 'band'), 'ga'), parts along dimension 0
There are 2 independent parts, one for each index of `img`. A program takes and returns all parts, laid end to end along the dimension named above; an argument that names none is the same for every part. Nothing has to cross between parts.
Inputs may be any that keep to these rules, and one draw needn't show every extreme that they name: `orbitals`: the bands of one image are linearly independent, and the block lies largely in their span.
All inputs are finite; a program needn't handle non-finite values.
Results may differ from a plain program's by a relative error of at most 0.02.
Values may be sent and summed in bfloat16 or wider, within the bound.
A program may use at most 64 MiB of HBM per device.

v0:
```python
import jax
import jax.numpy as jnp
from jax import lax
from jax.sharding import PartitionSpec as P


def over_pieces(shard, axis):
    pieces = lax.all_gather(shard, axis).astype(jnp.float32)
    return pieces.sum(axis=0)


def from_everyone(shard, axis):
    count = lax.axis_size(axis)
    return lax.all_to_all(
        jnp.broadcast_to(shard[None], (count, *shard.shape)), axis, 0, 0, tiled=True
    )


def in_order(pieces, dim):
    pieces = jnp.moveaxis(pieces, 0, dim)
    dims = pieces.shape
    return pieces.reshape(*dims[:dim], dims[dim] * dims[dim + 1], *dims[dim + 2 :])


def gathered_copies(shard, axis, dim):
    pieces = from_everyone(shard, axis)
    return in_order(pieces, dim)


def taken_together(shard, axis):
    return from_everyone(shard, axis).astype(jnp.float32).sum(axis=0)


def cut_along(shard, dim, count):
    dims = shard.shape
    pieces = shard.reshape(*dims[:dim], count, dims[dim] // count, *dims[dim + 1 :])
    return jnp.moveaxis(pieces, dim, 0)


def sent_and_summed(shard, axis, dim):
    pieces = cut_along(shard, dim, lax.axis_size(axis))
    arrived = lax.all_to_all(pieces, axis, split_axis=0, concat_axis=0, tiled=True)
    return arrived.astype(jnp.float32).sum(axis=0)


def contract_first(left, right):
    return lax.dot_general(left, right, (((0,), (0,)), ((), ())), precision=lax.Precision.HIGHEST)


def shards(orbitals, kernel, block_vectors):
    groups = lax.axis_size("ga")
    own_band = lax.axis_index("band")
    total_coeffs = orbitals.shape[1] * groups
    full_orbitals, full_block = (
        lax.all_gather(orbitals, "band", axis=0, tiled=True),
        lax.all_gather(block_vectors, "band", axis=0, tiled=True),
    )
    weighted = (-(full_orbitals.astype(jnp.float32) * kernel[None, :])).astype(jnp.bfloat16)
    own_rows = orbitals.shape[0]
    partial_rows = lax.dot_general(
        orbitals, weighted, (((1,), (1,)), ((), ())), preferred_element_type=jnp.float32
    )
    summed_rows = over_pieces(partial_rows.astype(jnp.bfloat16), "ga").astype(jnp.float32)
    margin = (
        -gathered_copies(summed_rows.astype(jnp.bfloat16), "band", 0).astype(summed_rows.dtype)
        / total_coeffs
    )
    factor = jnp.linalg.cholesky(margin)
    identity = jnp.eye(factor.shape[0], dtype=jnp.float32)
    inverse = lax.linalg.triangular_solve(factor, identity, left_side=True, lower=True)
    inverse_rows = lax.dynamic_slice_in_dim(inverse, own_band * own_rows, own_rows, 0)
    projector = jnp.dot(inverse_rows, weighted.astype(jnp.float32), precision=lax.Precision.HIGHEST)
    local_coupling = jnp.dot(
        projector, full_block.astype(jnp.float32).T, precision=lax.Precision.HIGHEST
    )
    coupling = (
        taken_together(local_coupling.astype(jnp.bfloat16), "ga").astype(jnp.float32) / total_coeffs
    )
    applied = sent_and_summed(
        (-contract_first(coupling, projector)).astype(jnp.bfloat16), "band", 0
    )
    return (projector.astype(jnp.bfloat16), applied.astype(jnp.bfloat16))


def solution(mesh):
    placed = (P(("img", "band"), "ga"), P("ga"), P(("img", "band"), "ga"))
    return jax.shard_map(
        shards,
        mesh=mesh,
        in_specs=placed,
        out_specs=(P(("img", "band"), "ga"), P(("img", "band"), "ga")),
        check_vma=False,
    )
```

profile of v0, /device:TPU:513, one launch (start us, length us, event | category | flops | bytes accessed | tf_op | source)
XLA Modules:
  0.0 510.3 jit_solution(14080767505893318742)
XLA Ops:
  8.0 80.9 %all-gather.5.cloned.1.call-done = bf16[768,3072]{1,0:T(8,128)(2,1)} async-done(((bf16[96,3072]{1,0:T(8,128)(2,1)}), bf16[768,3072]{1,0:T(8,128)(2,1)}) %all-gather.5.cloned.1.call-update) | async-done | bytes 4718608 | tf_op jit(solution)/shard_map/all_gather | solution.py:55
  89.0 4.8 fusion.21
  93.8 41.2 %all-gather.9.cloned.1.call-done = bf16[1536,768]{1,0:T(8,128)(2,1)} async-done(((bf16[96,768]{1,0:T(8,128)(2,1)}), bf16[1536,768]{1,0:T(8,128)(2,1)}) %all-gather.9.cloned.1.call-update) | async-done | bytes 2359312 | tf_op jit(solution)/shard_map/all_gather | solution.py:8
  134.9 2.0 reduce_sum.33
  136.9 1.1 broadcast_in_dim.5
  138.0 6.4 %all-to-all-start = ((bf16[8,96,768]{2,1,0:T(8,128)(2,1)}), bf16[8,96,768]{2,1,0:T(8,128)(2,1)S(1)}, u32[]{:S(2)}, u32[]{:S(2)}) async-start(bf16[8,96,768]{2,1,0:T(8,128)(2,1)} %broadcast_in_dim.5), calls=%async_computation | async-start | bytes 2359296 | tf_op jit(solution)/shard_map/all_to_all | solution.py:14
  146.3 1.6 fusion.25
  147.9 35.2 %all-to-all-done = bf16[8,96,768]{2,1,0:T(8,128)(2,1)S(1)} async-done(((bf16[8,96,768]{2,1,0:T(8,128)(2,1)}), bf16[8,96,768]{2,1,0:T(8,128)(2,1)S(1)}, u32[]{:S(2)}, u32[]{:S(2)}) %all-to-all-start) | async-done | bytes 1179680 | tf_op jit(solution)/shard_map/all_to_all | solution.py:14
  183.3 2.2 copy.7
  185.5 1.9 fusion.3
  187.4 1.5 copy-done.1
  188.9 11.7 %cholesky.165 = f32[128,128]{1,0:T(8,128)S(1)} custom-call(f32[128,128]{1,0:T(8,128)S(1)} %cholesky.424), custom_call_target="Cholesky" | custom-call | tf_op jit(solution)/shard_map/jit(cholesky)/cholesky | solution.py:68
  200.6 9.8 %custom-call.46 = f32[1,128,128]{1,2,0:T(8,128)S(1)} custom-call(f32[1,128,128]{2,1,0:T(8,128)S(1)} %get-tuple-element.45), custom_call_target="InvertDiagBlocksLowerTriangular" | custom-call | tf_op jit(solution)/shard_map/jit(cholesky)/cholesky | solution.py:68
  210.6 1.4 constant_dynamic-update-slice_fusion.15
  212.0 1.4 convolution_subtract_fusion.4
  213.4 11.7 %cholesky.188 = f32[128,128]{1,0:T(8,128)S(1)} custom-call(f32[128,128]{1,0:T(8,128)S(1)} %cholesky.428), custom_call_target="Cholesky" | custom-call | tf_op jit(solution)/shard_map/jit(cholesky)/cholesky | solution.py:68
  225.2 10.0 %custom-call.47 = f32[1,128,128]{1,2,0:T(8,128)S(1)} custom-call(f32[1,128,128]{2,1,0:T(8,128)S(1)} %get-tuple-element.42), custom_call_target="InvertDiagBlocksLowerTriangular" | custom-call | tf_op jit(solution)/shard_map/jit(cholesky)/cholesky | solution.py:68
  235.5 1.5 convolution_subtract_fusion.5
  237.1 11.7 %cholesky.354 = f32[128,128]{1,0:T(8,128)S(1)} custom-call(f32[128,128]{1,0:T(8,128)S(1)} %cholesky.433), custom_call_target="Cholesky" | custom-call | tf_op jit(solution)/shard_map/jit(cholesky)/cholesky | solution.py:68
  249.5 9.8 %custom-call.48 = f32[1,128,128]{1,2,0:T(8,128)S(1)} custom-call(f32[1,128,128]{2,1,0:T(8,128)S(1)} %get-tuple-element.39), custom_call_target="InvertDiagBlocksLowerTriangular" | custom-call | tf_op jit(solution)/shard_map/jit(cholesky)/cholesky | solution.py:68
  259.7 1.6 convolution_subtract_fusion.6
  261.2 12.2 %cholesky.373 = f32[128,128]{1,0:T(8,128)S(1)} custom-call(f32[128,128]{1,0:T(8,128)S(1)} %cholesky.438), custom_call_target="Cholesky" | custom-call | tf_op jit(solution)/shard_map/jit(cholesky)/cholesky | solution.py:68
  274.1 9.8 %custom-call.49 = f32[1,128,128]{1,2,0:T(8,128)S(1)} custom-call(f32[1,128,128]{2,1,0:T(8,128)S(1)} %get-tuple-element.36), custom_call_target="InvertDiagBlocksLowerTriangular" | custom-call | tf_op jit(solution)/shard_map/jit(cholesky)/cholesky | solution.py:68
  284.2 1.5 convolution_subtract_fusion.7
  285.7 11.7 %cholesky.392 = f32[128,128]{1,0:T(8,128)S(1)} custom-call(f32[128,128]{1,0:T(8,128)S(1)} %cholesky.443), custom_call_target="Cholesky" | custom-call | tf_op jit(solution)/shard_map/jit(cholesky)/cholesky | solution.py:68
  298.2 9.8 %custom-call.50 = f32[1,128,128]{1,2,0:T(8,128)S(1)} custom-call(f32[1,128,128]{2,1,0:T(8,128)S(1)} %get-tuple-element.33), custom_call_target="InvertDiagBlocksLowerTriangular" | custom-call | tf_op jit(solution)/shard_map/jit(cholesky)/cholesky | solution.py:68
  308.2 1.3 convolution_subtract_fusion.8
  309.5 11.9 %cholesky.410 = f32[128,128]{1,0:T(8,128)S(1)} custom-call(f32[128,128]{1,0:T(8,128)S(1)} %convolution_subtract_fusion.8), custom_call_target="Cholesky" | custom-call | tf_op jit(solution)/shard_map/jit(cholesky)/cholesky | solution.py:68
  326.5 1.6 select_select_fusion
  328.2 21.5 %while.1 = (s32[]{:T(128)}, f32[768,768]{1,0:T(8,128)}, s32[6,2]{0,1:T(2,128)S(1)}, f32[6,128,128]{2,1,0:T(8,128)}, s32[]{:T(128)}) while((s32[]{:T(128)}, f32[768,768]{1,0:T(8,128)}, s32[6,2]{0,1:T(2,128)S(1)}, f32[6,128,128]{2,1,0:T(8,128)}, s32[]{:T(128)}) %tuple.45), condition=%wide.while_cond, body=%wide.while_body.sunk | while | flops 2 | bytes 132705 | solution.py:70
  328.8 2.9 bitcast_dynamic-update-slice_fusion.2
  332.5 2.9 bitcast_dynamic-update-slice_fusion.2
  336.1 2.9 bitcast_dynamic-update-slice_fusion.2
  339.6 2.9 bitcast_dynamic-update-slice_fusion.2
  343.2 2.9 bitcast_dynamic-update-slice_fusion.2
  346.8 2.8 bitcast_dynamic-update-slice_fusion.2
  349.7 59.8 %custom-call.51 = f32[6,128,128]{1,2,0:T(8,128)S(1)} custom-call(f32[6,128,128]{2,1,0:T(8,128)} %get-tuple-element.9), custom_call_target="InvertDiagBlocksLowerTriangular" | custom-call | tf_op jit(solution)/shard_map/triangular_solve | solution.py:70
  409.4 1.2 constant_dynamic-update-slice_fusion.4
  410.6 1.5 convolution_subtract_fusion.2
  412.7 1.5 convolution_subtract_fusion.3
  414.7 2.0 convolution_subtract_fusion.1
  417.2 2.0 fusion.12
  419.8 2.3 convolution_subtract_fusion
  422.6 3.7 fusion.65
  426.4 3.0 convolution_convert_fusion
  429.4 27.4 %all_to_all.15 = bf16[16,96,256]{2,1,0:T(8,128)(2,1)S(1)} all-to-all(bf16[16,96,256]{2,1,0:T(8,128)(2,1)S(1)} %broadcast_in_dim.7), channel_id=1, replica_groups=mesh['img'=2,'ga'=16,'band'=8] {'ga'}, dimensions={0} | all-to-all | bytes 1572864 | tf_op jit(solution)/shard_map/all_to_all | solution.py:14
  456.9 2.7 fusion
  459.6 43.0 %all_to_all.16 = bf16[8,32,3072]{2,1,0:T(8,128)(2,1)S(1)} all-to-all(bf16[8,32,3072]{2,1,0:T(8,128)(2,1)S(1)} %bitcast.88), channel_id=1, replica_groups=mesh['img'=2,'ga'=16,'band'=8] {'band'}, dimensions={0} | all-to-all | bytes 3145728 | tf_op jit(solution)/shard_map/all_to_all | solution.py:42
  (63 shorter events, 15.6 us)
Async XLA Ops:
  7.2 81.8 %all-gather.5.cloned.1.call-start = ((), (), s32[]{:S(2)}) async-start(), calls=%async_computation.3 | async-start | bytes 5308416 | tf_op jit(solution)/shard_map/all_gather | solution.py:55
  8.0 127.0 %all-gather.9.cloned.1.call-start = ((), (), s32[]{:S(2)}) async-start(), calls=%async_computation.5 | async-start | bytes 2506752 | tf_op jit(solution)/shard_map/all_gather | solution.py:8
  138.0 45.0 %all-to-all-start = ((bf16[8,96,768]{2,1,0:T(8,128)(2,1)}), bf16[8,96,768]{2,1,0:T(8,128)(2,1)S(1)}, u32[]{:S(2)}, u32[]{:S(2)}) async-start(bf16[8,96,768]{2,1,0:T(8,128)(2,1)} %broadcast_in_dim.5), calls=%async_computation | async-start | bytes 2359296 | tf_op jit(solution)/shard_map/all_to_all | solution.py:14
  144.5 281.9 %all-gather.7.cloned.1.call-start = ((), (), s32[]{:S(2)}) async-start(), calls=%async_computation.4 | async-start | bytes 1769472 | tf_op jit(solution)/shard_map/all_gather | solution.py:56
  187.4 1.5 copy-start.1
  328.2 84.5 %copy-start = (f32[768,768]{1,0:T(8,128)S(1)}, f32[768,768]{1,0:T(8,128)}, u32[]{:S(2)}) copy-start(f32[768,768]{1,0:T(8,128)} %fusion.25) | copy-start | bytes 7077892
  414.7 7.9 %slice-start = ((s8[4718592]{0:T(1024)(128)(4,1)}), s8[4194304]{0:T(1024)(128)(4,1)S(1)}, s32[]{:S(2)}) async-start(s8[4718592]{0:T(1024)(128)(4,1)} %bitcast.90), calls=%async_computation.6 | async-start | bytes 8388608
  417.2 5.4 %slice-start.1 = ((s8[4718592]{0:T(1024)(128)(4,1)}), s8[524288]{0:T(1024)(128)(4,1)S(1)}, s32[]{:S(2)}) async-start(s8[4718592]{0:T(1024)(128)(4,1)} %bitcast.90), calls=%async_computation.7 | async-start | bytes 1048576
  419.2 3.4 copy-start.2
Sparse Core Ops, SparseCore 0:
  9.8 79.1 all-gather.4
  93.9 40.9 all-gather.8
  147.1 44.9 all-gather.6
where the time goes:
time: 514 us; the launch traced here: 510 us
  other arithmetic  193 us (38%)
  waiting for transfers between devices  159 us (31%)
  blocking collectives  70.4 us (14%)
  matrix products  37 us (7%)
  local copies, waits for them, and re-layouts  26.5 us (5%)
  between operations  18.2 us (4%)
  starting transfers between devices  6.6 us (1%)
    another operation x22, other arithmetic, shards(): factor = jnp.linalg.cholesky(margin)  124 us
    all_gather x1, waiting for transfers between devices, shards(): lax.all_gather(orbitals, 'band', axis=0, tiled=True)  80.9 us
    another operation x3, other arithmetic, shards(): lax.linalg.triangular_solve(factor, identity, left_side=True, lower=True)  61.4 us
    all_to_all x1, blocking collectives, sent_and_summed(): lax.all_to_all(pieces, axis, split_axis=0, concat_axis=0, tiled=True)  43 us
    all_gather x1, waiting for transfers between devices, over_pieces(): pieces = lax.all_gather(shard, axis).astype(jnp.float32)  41.2 us
    all_to_all x1, waiting for transfers between devices, from_everyone(): lax.all_to_all(jnp.broadcast_to(shard[None], (count, *shard.shape)), axis...  35.2 us
    all_to_all x1, blocking collectives, from_everyone(): lax.all_to_all(jnp.broadcast_to(shard[None], (count, *shard.shape)), axis...  27.4 us
    another operation x18, local copies, waits for them, and re-layouts  21.5 us
  transfers between devices with their start and end apart: 4, of which 3 were waited for; matrix products, arithmetic and copies ran while one was open for 47% of the time, Pallas kernels for 0%

commit v1 on v0

--- a/solution.py
+++ b/solution.py
@@ -2,6 +2,11 @@
 import jax.numpy as jnp
 from jax import lax
 from jax.sharding import PartitionSpec as P
+
+
+def tiled_gather(x, axis, dim):
+    copies = jnp.concatenate([x] * lax.axis_size(axis), axis=dim)
+    return lax.all_to_all(copies, axis, dim, dim, tiled=True)
 
 
 def over_pieces(shard, axis):
@@ -52,7 +57,7 @@
     own_band = lax.axis_index("band")
     total_coeffs = orbitals.shape[1] * groups
     full_orbitals, full_block = (
-        lax.all_gather(orbitals, "band", axis=0, tiled=True),
+        tiled_gather(orbitals, "band", 0),
         lax.all_gather(block_vectors, "band", axis=0, tiled=True),
     )
     weighted = (-(full_orbitals.astype(jnp.float32) * kernel[None, :])).astype(jnp.bfloat16)

time: 514 us -> 568 us (1.11)
  blocking collectives: 70.4 us -> 170 us
  waiting for transfers between devices: 159 us -> 106 us
    all_to_all x0 -> x1, blocking collectives: none -> 99.4 us  [tiled_gather(): return lax.all_to_all(copies, axis, dim, dim, tiled=True)]
    all_gather x1 -> x0, waiting for transfers between devices: 80.9 us -> none  [shards(): lax.all_gather(orbitals, 'band', axis=0, tiled=True)]
    all_gather x1, waiting for transfers between devices: 41.2 us -> 70.3 us  [over_pieces(): pieces = lax.all_gather(shard, axis).astype(jnp.float32)]
  transfers between devices with their start and end apart: 4 -> 3, of which waited for: 3 -> 2; matrix products, arithmetic and copies ran while one was open for 47% -> 43% of each run, Pallas kernels for 0% -> 0%
where the time goes in v1:
time: 568 us; the launch traced here: 562 us
  other arithmetic  194 us (34%)
  blocking collectives  170 us (30%)
  waiting for transfers between devices  106 us (19%)
  matrix products  34 us (6%)
  local copies, waits for them, and re-layouts  31.2 us (5%)
  between operations  20.2 us (4%)
  starting transfers between devices  6.54 us (1%)
    another operation x22, other arithmetic, shards(): factor = jnp.linalg.cholesky(margin)  124 us
    all_to_all x1, blocking collectives, tiled_gather(): return lax.all_to_all(copies, axis, dim, dim, tiled=True)  99.4 us
    all_gather x1, waiting for transfers between devices, over_pieces(): pieces = lax.all_gather(shard, axis).astype(jnp.float32)  70.3 us
    another operation x3, other arithmetic, shards(): lax.linalg.triangular_solve(factor, identity, left_side=True, lower=True)  61.4 us
    all_to_all x1, blocking collectives, sent_and_summed(): lax.all_to_all(pieces, axis, split_axis=0, concat_axis=0, tiled=True)  42.9 us
    all_to_all x1, waiting for transfers between devices, from_everyone(): lax.all_to_all(jnp.broadcast_to(shard[None], (count, *shard.shape)), axis...  35.6 us
    all_to_all x1, blocking collectives, from_everyone(): lax.all_to_all(jnp.broadcast_to(shard[None], (count, *shard.shape)), axis...  27.4 us
    another operation x18, local copies, waits for them, and re-layouts  21.5 us
  transfers between devices with their start and end apart: 3, of which 2 were waited for; matrix products, arithmetic and copies ran while one was open for 43% of the time, Pallas kernels for 0%

profile of v1, /device:TPU:513, one launch (start us, length us, event | category | flops | bytes accessed | tf_op | source)
XLA Modules:
  0.0 562.4 jit_solution(13178203216048389176)
XLA Ops:
  10.7 99.4 %all_to_all.24 = bf16[8,96,3072]{2,1,0:T(8,128)(2,1)S(1)} all-to-all(bf16[8,96,3072]{2,1,0:T(8,128)(2,1)S(1)} %bitcast.97), channel_id=1, replica_groups=mesh['img'=2,'ga'=16,'band'=8] {'band'}, dimensions={0} | all-to-all | bytes 9437184 | tf_op jit(solution)/shard_map/all_to_all | solution.py:9
  110.1 1.5 fusion.1
  111.6 2.1 copy-done.1
  113.7 2.3 fusion.20
  116.1 70.3 %all-gather.6.cloned.1.call-done = bf16[1536,768]{1,0:T(8,128)(2,1)} async-done(((bf16[96,768]{1,0:T(8,128)(2,1)}), bf16[1536,768]{1,0:T(8,128)(2,1)}) %all-gather.6.cloned.1.call-update) | async-done | bytes 2359312 | tf_op jit(solution)/shard_map/all_gather | solution.py:13
  186.4 2.0 reduce_sum.33
  189.5 6.4 %all-to-all-start.1 = ((bf16[8,96,768]{2,1,0:T(8,128)(2,1)}), bf16[8,96,768]{2,1,0:T(8,128)(2,1)S(1)}, u32[]{:S(2)}, u32[]{:S(2)}) async-start(bf16[8,96,768]{2,1,0:T(8,128)(2,1)} %broadcast_in_dim.5), calls=%async_computation.1 | async-start | bytes 2359296 | tf_op jit(solution)/shard_map/all_to_all | solution.py:19
  197.5 1.6 fusion.24
  199.1 35.6 %all-to-all-done.1 = bf16[8,96,768]{2,1,0:T(8,128)(2,1)S(1)} async-done(((bf16[8,96,768]{2,1,0:T(8,128)(2,1)}), bf16[8,96,768]{2,1,0:T(8,128)(2,1)S(1)}, u32[]{:S(2)}, u32[]{:S(2)}) %all-to-all-start.1) | async-done | bytes 1179680 | tf_op jit(solution)/shard_map/all_to_all | solution.py:19
  234.9 2.2 copy.7
  237.2 1.9 fusion.3
  239.1 1.5 copy-done.3
  240.6 11.7 %cholesky.165 = f32[128,128]{1,0:T(8,128)S(1)} custom-call(f32[128,128]{1,0:T(8,128)S(1)} %cholesky.424), custom_call_target="Cholesky" | custom-call | tf_op jit(solution)/shard_map/jit(cholesky)/cholesky | solution.py:73
  252.3 9.8 %custom-call.46 = f32[1,128,128]{1,2,0:T(8,128)S(1)} custom-call(f32[1,128,128]{2,1,0:T(8,128)S(1)} %get-tuple-element.45), custom_call_target="InvertDiagBlocksLowerTriangular" | custom-call | tf_op jit(solution)/shard_map/jit(cholesky)/cholesky | solution.py:73
  262.3 1.4 constant_dynamic-update-slice_fusion.23
  263.7 1.4 convolution_subtract_fusion.4
  265.1 11.7 %cholesky.188 = f32[128,128]{1,0:T(8,128)S(1)} custom-call(f32[128,128]{1,0:T(8,128)S(1)} %cholesky.428), custom_call_target="Cholesky" | custom-call | tf_op jit(solution)/shard_map/jit(cholesky)/cholesky | solution.py:73
  276.8 10.2 %custom-call.47 = f32[1,128,128]{1,2,0:T(8,128)S(1)} custom-call(f32[1,128,128]{2,1,0:T(8,128)S(1)} %get-tuple-element.42), custom_call_target="InvertDiagBlocksLowerTriangular" | custom-call | tf_op jit(solution)/shard_map/jit(cholesky)/cholesky | solution.py:73
  287.4 1.5 convolution_subtract_fusion.5
  289.0 11.7 %cholesky.354 = f32[128,128]{1,0:T(8,128)S(1)} custom-call(f32[128,128]{1,0:T(8,128)S(1)} %cholesky.433), custom_call_target="Cholesky" | custom-call | tf_op jit(solution)/shard_map/jit(cholesky)/cholesky | solution.py:73
  301.4 9.8 %custom-call.48 = f32[1,128,128]{1,2,0:T(8,128)S(1)} custom-call(f32[1,128,128]{2,1,0:T(8,128)S(1)} %get-tuple-element.39), custom_call_target="InvertDiagBlocksLowerTriangular" | custom-call | tf_op jit(solution)/shard_map/jit(cholesky)/cholesky | solution.py:73
  311.6 1.6 convolution_subtract_fusion.6
  313.1 11.9 %cholesky.373 = f32[128,128]{1,0:T(8,128)S(1)} custom-call(f32[128,128]{1,0:T(8,128)S(1)} %cholesky.438), custom_call_target="Cholesky" | custom-call | tf_op jit(solution)/shard_map/jit(cholesky)/cholesky | solution.py:73
  325.7 9.8 %custom-call.49 = f32[1,128,128]{1,2,0:T(8,128)S(1)} custom-call(f32[1,128,128]{2,1,0:T(8,128)S(1)} %get-tuple-element.36), custom_call_target="InvertDiagBlocksLowerTriangular" | custom-call | tf_op jit(solution)/shard_map/jit(cholesky)/cholesky | solution.py:73
  335.8 1.5 convolution_subtract_fusion.7
  337.3 11.7 %cholesky.392 = f32[128,128]{1,0:T(8,128)S(1)} custom-call(f32[128,128]{1,0:T(8,128)S(1)} %cholesky.443), custom_call_target="Cholesky" | custom-call | tf_op jit(solution)/shard_map/jit(cholesky)/cholesky | solution.py:73
  349.7 9.8 %custom-call.50 = f32[1,128,128]{1,2,0:T(8,128)S(1)} custom-call(f32[1,128,128]{2,1,0:T(8,128)S(1)} %get-tuple-element.33), custom_call_target="InvertDiagBlocksLowerTriangular" | custom-call | tf_op jit(solution)/shard_map/jit(cholesky)/cholesky | solution.py:73
  359.8 1.3 convolution_subtract_fusion.8
  361.1 11.9 %cholesky.410 = f32[128,128]{1,0:T(8,128)S(1)} custom-call(f32[128,128]{1,0:T(8,128)S(1)} %convolution_subtract_fusion.8), custom_call_target="Cholesky" | custom-call | tf_op jit(solution)/shard_map/jit(cholesky)/cholesky | solution.py:73
  378.2 1.6 select_select_fusion
  379.8 21.5 %while.1 = (s32[]{:T(128)}, f32[768,768]{1,0:T(8,128)}, s32[6,2]{0,1:T(2,128)S(1)}, f32[6,128,128]{2,1,0:T(8,128)}, s32[]{:T(128)}) while((s32[]{:T(128)}, f32[768,768]{1,0:T(8,128)}, s32[6,2]{0,1:T(2,128)S(1)}, f32[6,128,128]{2,1,0:T(8,128)}, s32[]{:T(128)}) %tuple.45), condition=%wide.while_cond, body=%wide.while_body.sunk | while | flops 2 | bytes 132705 | solution.py:75
  380.5 2.9 bitcast_dynamic-update-slice_fusion.2
  384.1 2.9 bitcast_dynamic-update-slice_fusion.2
  387.7 2.9 bitcast_dynamic-update-slice_fusion.2
  391.3 2.9 bitcast_dynamic-update-slice_fusion.2
  394.9 2.9 bitcast_dynamic-update-slice_fusion.2
  398.4 2.8 bitcast_dynamic-update-slice_fusion.2
  401.3 59.8 %custom-call.51 = f32[6,128,128]{1,2,0:T(8,128)S(1)} custom-call(f32[6,128,128]{2,1,0:T(8,128)} %get-tuple-element.9), custom_call_target="InvertDiagBlocksLowerTriangular" | custom-call | tf_op jit(solution)/shard_map/triangular_solve | solution.py:75
  462.2 1.5 convolution_subtract_fusion.2
  464.3 1.5 convolution_subtract_fusion.3
  466.3 2.0 convolution_subtract_fusion.1
  468.8 2.0 fusion.12
  471.4 2.3 convolution_subtract_fusion
  474.2 3.2 fusion.65
  477.5 3.0 convolution_convert_fusion.1
  480.5 27.4 %all_to_all.25 = bf16[16,96,256]{2,1,0:T(8,128)(2,1)S(1)} all-to-all(bf16[16,96,256]{2,1,0:T(8,128)(2,1)S(1)} %broadcast_in_dim.7), channel_id=1, replica_groups=mesh['img'=2,'ga'=16,'band'=8] {'ga'}, dimensions={0} | all-to-all | bytes 1572864 | tf_op jit(solution)/shard_map/all_to_all | solution.py:19
  508.0 2.7 fusion.2
  510.7 42.9 %all_to_all.26 = bf16[8,32,3072]{2,1,0:T(8,128)(2,1)S(1)} all-to-all(bf16[8,32,3072]{2,1,0:T(8,128)(2,1)S(1)} %bitcast.96), channel_id=1, replica_groups=mesh['img'=2,'ga'=16,'band'=8] {'band'}, dimensions={0} | all-to-all | bytes 3145728 | tf_op jit(solution)/shard_map/all_to_all | solution.py:47
  (74 shorter events, 19.5 us)
Async XLA Ops:
  8.0 2.3 copy-start
  8.0 178.3 %all-gather.6.cloned.1.call-start = ((), (), s32[]{:S(2)}) async-start(), calls=%async_computation.5 | async-start | bytes 2506752 | tf_op jit(solution)/shard_map/all_gather | solution.py:13
  10.7 99.4 %copy-start.4 = (f32[3072]{0:T(1024)S(1)}, f32[3072]{0:T(1024)}, u32[]{:S(2)}) copy-start(f32[3072]{0:T(1024)} %param.4) | copy-start | bytes 36868
  111.6 2.1 copy-start.1
  189.5 45.2 %all-to-all-start.1 = ((bf16[8,96,768]{2,1,0:T(8,128)(2,1)}), bf16[8,96,768]{2,1,0:T(8,128)(2,1)S(1)}, u32[]{:S(2)}, u32[]{:S(2)}) async-start(bf16[8,96,768]{2,1,0:T(8,128)(2,1)} %broadcast_in_dim.5), calls=%async_computation.1 | async-start | bytes 2359296 | tf_op jit(solution)/shard_map/all_to_all | solution.py:19
  195.9 281.6 %all-gather.4.cloned.1.call-start = ((), (), s32[]{:S(2)}) async-start(), calls=%async_computation.4 | async-start | bytes 1769472 | tf_op jit(solution)/shard_map/all_gather | solution.py:61
  239.1 1.5 copy-start.3
  379.8 84.5 %copy-start.2 = (f32[768,768]{1,0:T(8,128)S(1)}, f32[768,768]{1,0:T(8,128)}, u32[]{:S(2)}) copy-start(f32[768,768]{1,0:T(8,128)} %fusion.24) | copy-start | bytes 7077892
  466.3 7.9 %slice-start = ((s8[4718592]{0:T(1024)(128)(4,1)}), s8[4194304]{0:T(1024)(128)(4,1)S(1)}, s32[]{:S(2)}) async-start(s8[4718592]{0:T(1024)(128)(4,1)} %bitcast.93), calls=%async_computation.6 | async-start | bytes 8388608
  468.8 5.4 slice-start.1
Sparse Core Ops, SparseCore 0:
  116.2 70.1 all-gather.5
Sparse Core Ops, SparseCore 1:
  198.2 45.3 all-gather.3
